TPU v7x, 32 devices: a whole 2x2x4 slice. The times are simulated.
32 devices in a mesh: unit: 4 (over y, x), north: 4 (over z), east: 2 (over core).
Axes of the slice: x: 2, y: 2, z: 4, core: 2. Of those that a mesh axis runs over, the one named last changes fastest.
Arguments:
- pair_rows: bfloat16 [256, 64, 128], P(('unit', 'north'), 'east'), parts along dimension 0, may hold values from -6 to 6
- in_gain: float32 [128], replicated, may hold values from 0.25 to 1.75
- left_weight: bfloat16 [512, 128], P('unit'), parts along dimension 0, may hold values from -0.5 to 0.5
- right_weight: bfloat16 [512, 128], P('unit'), parts along dimension 0, may hold values from -0.5 to 0.5
- left_gate: bfloat16 [512, 128], P('unit'), parts along dimension 0, may hold values from -0.5 to 0.5
- right_gate: bfloat16 [512, 128], P('unit'), parts along dimension 0, may hold values from -0.5 to 0.5
- mid_gain: float32 [128], replicated, may hold values from 0.25 to 1.75
- out_weight: bfloat16 [512, 128], P('unit'), parts along dimension 0, may hold values from -0.5 to 0.5
- out_gate: bfloat16 [512, 128], P('unit'), parts along dimension 0, may hold values from -0.5 to 0.5
Outputs:
- triangle_out: bfloat16 [256, 64, 128], P(('unit', 'north'), 'east'), parts along dimension 0
There are 4 independent parts, one for each index of `unit`. A program takes and returns all parts, laid end to end along the dimension named above; an argument that names none is the same for every part. Nothing has to cross between parts.
All inputs are finite; a program needn't handle non-finite values.
Results may differ from a plain program's by a relative error of at most 0.015.
Values may be sent and summed in bfloat16 or wider, within the bound.
A program may use at most 128 MiB of HBM per device.

v0:
```python
import jax
import jax.numpy as jnp
from jax import lax
from jax.sharding import PartitionSpec as P


def over_all(piece, axis, dim, apply):
    everything = lax.all_gather(piece, axis, axis=dim, tiled=True)
    return apply(everything, jnp.int32(0))


def scale_channels(values, channel_gain):
    centred = values - jnp.mean(values, axis=-1, keepdims=True)
    return (
        centred
        * lax.rsqrt(jnp.mean(centred * centred, axis=-1, keepdims=True) + 1e-05)
        * channel_gain
    )


def make_factors(pair_in, in_gain, left_weight, right_weight, left_gate, right_gate):
    ready = scale_channels(pair_in.astype(jnp.float32), in_gain).astype(jnp.bfloat16)
    ready = lax.optimization_barrier(ready)
    left = jnp.einsum("ijc,cd->ijd", ready, left_weight, preferred_element_type=jnp.float32)
    left = left * jax.nn.sigmoid(
        jnp.einsum("ijc,cd->ijd", ready, left_gate, preferred_element_type=jnp.float32)
    )
    right = jnp.einsum("ijc,cd->ijd", ready, right_weight, preferred_element_type=jnp.float32)
    right = right * jax.nn.sigmoid(
        jnp.einsum("ijc,cd->ijd", ready, right_gate, preferred_element_type=jnp.float32)
    )
    return (ready, left.astype(jnp.bfloat16), right.astype(jnp.bfloat16))


def finish_pair(mixed, ready, mid_gain, out_weight, out_gate):
    scaled = scale_channels(mixed.astype(jnp.float32), mid_gain).astype(jnp.bfloat16)
    scaled = lax.optimization_barrier(scaled)
    gate = jax.nn.sigmoid(
        jnp.einsum("ijc,cd->ijd", ready, out_gate, preferred_element_type=jnp.float32)
    )
    return (
        jnp.einsum("ijd,dc->ijc", scaled, out_weight, preferred_element_type=jnp.float32) * gate
    ).astype(jnp.bfloat16)


def body(
    pair_rows,
    in_gain,
    left_weight,
    right_weight,
    left_gate,
    right_gate,
    mid_gain,
    out_weight,
    out_gate,
):
    ready, left, right = make_factors(
        pair_rows, in_gain, left_weight, right_weight, left_gate, right_gate
    )
    count = pair_rows.shape[0] * lax.axis_size("north")
    left_lines, right_lines = (
        lax.all_to_all(left, "north", split_axis=2, concat_axis=0, tiled=True),
        lax.all_to_all(right, "north", split_axis=2, concat_axis=0, tiled=True),
    )

    def meet(piece, start):
        return jnp.einsum("kid,kjd->ijd", piece, right_lines, preferred_element_type=jnp.float32)

    strip = over_all(left_lines, "east", 1, meet)
    strip = (strip * count ** (-0.5)).astype(jnp.bfloat16)
    mixed = lax.all_to_all(strip, "north", split_axis=0, concat_axis=2, tiled=True)
    return finish_pair(mixed, ready, mid_gain, out_weight, out_gate)


def solution(mesh):
    placed = (
        P(("unit", "north"), "east", None),
        P(),
        P("unit", None),
        P("unit", None),
        P("unit", None),
        P("unit", None),
        P(),
        P("unit", None),
        P("unit", None),
    )
    return jax.shard_map(
        body,
        mesh=mesh,
        in_specs=placed,
        out_specs=P(("unit", "north"), "east", None),
        check_vma=False,
    )
```

profile of v0, /device:TPU:0, one launch (start us, length us, event | category | flops | bytes accessed | tf_op | source)
XLA Modules:
  0.0 45.4 jit_solution(5967632410699933416)
XLA Ops:
  0.0 1.1 %convert_reduce_fusion = f32[16,32]{1,0:T(8,128)S(1)} fusion(bf16[16,32,128]{2,1,0:T(8,128)(2,1)} %param.9), kind=kLoop, calls=%fused_computation.25 | loop fusion | flops 130560 | bytes 133120 | tf_op jit(solution)/shard_map/reduce_sum | solution.py:13
  1.4 0.6 %copy-done.5 = f32[128]{0:T(128)S(1)} copy-done((f32[128]{0:T(128)S(1)}, f32[128]{0:T(128)}, u32[]{:S(2)}) %copy-start.5) | copy-done | bytes 536
  2.5 0.5 %copy-done.2 = bf16[128,128]{1,0:T(8,128)(2,1)S(1)} copy-done((bf16[128,128]{1,0:T(8,128)(2,1)S(1)}, bf16[128,128]{1,0:T(8,128)(2,1)}, u32[]{:S(2)}) %copy-start.2) | copy-done | bytes 32792
  3.2 0.4 copy.27
  3.7 1.2 %reshape.43 = bf16[4,2,8192]{2,1,0:T(2,128)(2,1)} reshape(bf16[128,16,32]{2,1,0:T(8,128)(2,1)S(1)} %bitcast.53) | data formatting | bytes 262144
  4.8 6.5 %all-to-all-start.1 = ((bf16[4,2,8192]{2,1,0:T(2,128)(2,1)}), bf16[4,2,8192]{2,1,0:T(2,128)(2,1)S(1)}, u32[]{:S(2)}, u32[]{:S(2)}) async-start(bf16[4,2,8192]{2,1,0:T(2,128)(2,1)} %reshape.43), calls=%async_computation.1 | async-start | bytes 262144 | tf_op jit(solution)/shard_map/all_to_all | solution.py:62
  11.6 0.5 %copy-done.3 = bf16[128,128]{1,0:T(8,128)(2,1)S(1)} copy-done((bf16[128,128]{1,0:T(8,128)(2,1)S(1)}, bf16[128,128]{1,0:T(8,128)(2,1)}, u32[]{:S(2)}) %copy-start.3) | copy-done | bytes 32792
  12.7 1.2 %reshape.41 = bf16[4,2,8192]{2,1,0:T(2,128)(2,1)} reshape(bf16[128,16,32]{2,1,0:T(8,128)(2,1)S(1)} %bitcast.54) | data formatting | bytes 262144
  13.9 4.1 %all-to-all-done.1 = bf16[4,2,8192]{2,1,0:T(2,128)(2,1)S(1)} async-done(((bf16[4,2,8192]{2,1,0:T(2,128)(2,1)}), bf16[4,2,8192]{2,1,0:T(2,128)(2,1)S(1)}, u32[]{:S(2)}, u32[]{:S(2)}) %all-to-all-start.1) | async-done | bytes 131104 | tf_op jit(solution)/shard_map/all_to_all | solution.py:62
  18.0 3.3 %all-to-all-start = ((bf16[4,2,8192]{2,1,0:T(2,128)(2,1)}), bf16[4,2,8192]{2,1,0:T(2,128)(2,1)S(1)}, u32[]{:S(2)}, u32[]{:S(2)}) async-start(bf16[4,2,8192]{2,1,0:T(2,128)(2,1)} %reshape.41), calls=%async_computation | async-start | bytes 262144 | tf_op jit(solution)/shard_map/all_to_all | solution.py:63
  21.6 0.5 %copy.28 = bf16[16,32,4,32]{3,1,0,2:T(8,128)(2,1)S(1)} copy(bf16[16,32,4,32]{1,0,3,2:T(8,128)(2,1)S(1)} %bitcast.56) | data formatting | bytes 262144 | tf_op jit(solution)/shard_map/all_to_all | solution.py:62
  22.1 0.8 %copy.29 = bf16[64,32,32]{0,1,2:T(8,128)(2,1)S(1)} copy(bf16[64,32,32]{2,1,0:T(8,128)(2,1)S(1)} %bitcast.59) | data formatting | bytes 262144 | tf_op jit(solution)/shard_map/all_to_all | solution.py:62
  22.9 2.2 %all_gather.3 = bf16[64,64,32]{0,1,2:T(8,128)(2,1)S(1)} all-gather(bf16[64,32,32]{0,1,2:T(8,128)(2,1)S(1)} %copy.29), channel_id=1, replica_groups=mesh['unit'=4,'north'=4,'east'=2] {'east'}, dimensions={1}, use_global_device_ids=true | all-gather | bytes 393216 | tf_op jit(solution)/shard_map/all_gather | solution.py:8
  25.1 2.2 %all-to-all-done = bf16[4,2,8192]{2,1,0:T(2,128)(2,1)S(1)} async-done(((bf16[4,2,8192]{2,1,0:T(2,128)(2,1)}), bf16[4,2,8192]{2,1,0:T(2,128)(2,1)S(1)}, u32[]{:S(2)}, u32[]{:S(2)}) %all-to-all-start) | async-done | bytes 131104 | tf_op jit(solution)/shard_map/all_to_all | solution.py:63
  27.5 0.5 %copy.26 = bf16[16,32,4,32]{3,1,0,2:T(8,128)(2,1)S(1)} copy(bf16[16,32,4,32]{1,0,3,2:T(8,128)(2,1)S(1)} %bitcast.57) | data formatting | bytes 262144 | tf_op jit(solution)/shard_map/all_to_all | solution.py:63
  28.0 0.8 %copy.30 = bf16[64,32,32]{0,1,2:T(8,128)(2,1)S(1)} copy(bf16[64,32,32]{2,1,0:T(8,128)(2,1)S(1)} %bitcast.60) | data formatting | bytes 262144 | tf_op jit(solution)/shard_map/all_to_all | solution.py:63
  29.1 0.8 %copy.31 = bf16[64,32,32]{1,2,0:T(8,128)(2,1)S(1)} copy(bf16[64,32,32]{0,1,2:T(8,128)(2,1)S(1)} %fusion.10) | data formatting | bytes 262144 | tf_op jit(solution)/shard_map/convert_element_type | solution.py:70
  29.9 1.2 %reshape.45 = bf16[4,2,8192]{2,1,0:T(2,128)(2,1)} reshape(bf16[64,32,32]{2,1,0:T(8,128)(2,1)S(1)} %bitcast.55) | data formatting | bytes 262144
  31.1 3.5 %all-to-all-start.2 = ((bf16[4,2,8192]{2,1,0:T(2,128)(2,1)}), bf16[4,2,8192]{2,1,0:T(2,128)(2,1)S(1)}, u32[]{:S(2)}, u32[]{:S(2)}) async-start(bf16[4,2,8192]{2,1,0:T(2,128)(2,1)} %reshape.45), calls=%async_computation.2 | async-start | bytes 262144 | tf_op jit(solution)/shard_map/all_to_all | solution.py:71
  34.8 6.4 %all-to-all-done.2 = bf16[4,2,8192]{2,1,0:T(2,128)(2,1)S(1)} async-done(((bf16[4,2,8192]{2,1,0:T(2,128)(2,1)}), bf16[4,2,8192]{2,1,0:T(2,128)(2,1)S(1)}, u32[]{:S(2)}, u32[]{:S(2)}) %all-to-all-start.2) | async-done | bytes 131104 | tf_op jit(solution)/shard_map/all_to_all | solution.py:71
  42.4 0.7 %copy.33 = f32[16,32,4,32]{3,2,1,0:T(4,128)S(1)} copy(f32[16,32,4,32]{3,1,0,2:T(8,128)S(1)} %convert_bitcast_fusion) | data formatting | bytes 524288 | tf_op jit(solution)/shard_map/convert_element_type | solution.py:36
  43.1 0.5 %reshape.32 = f32[16,32,128]{2,1,0:T(8,128)S(1)} reshape(f32[16,32,4,32]{3,2,1,0:T(4,128)S(1)} %copy.33) | data formatting | bytes 524288 | tf_op jit(solution)/shard_map/convert_element_type | solution.py:36
  44.0 0.6 %copy-done.4 = bf16[128,128]{1,0:T(8,128)(2,1)S(1)} copy-done((bf16[128,128]{1,0:T(8,128)(2,1)S(1)}, bf16[128,128]{1,0:T(8,128)(2,1)}, u32[]{:S(2)}) %copy-start.4) | copy-done | bytes 32792
  44.5 0.8 %fusion.13 = bf16[16,32,128]{2,1,0:T(8,128)(2,1)} fusion(f32[16,32,128]{2,1,0:T(8,128)S(1)} %fusion.3, bf16[16,32,128]{2,1,0:T(8,128)(2,1)S(1)} %multiply_convert_fusion, bf16[128,128]{1,0:T(8,128)(2,1)S(1)} %copy-done.4), kind=kOutput, calls=%fused_computation.20 | convolution fusion | flops 16908288 | bytes 557056 | tf_op jit(solution)/shard_map/ijd,dc->ijc/dot_general | solution.py:42
  (35 shorter events, 4.3 us)
Async XLA Ops:
  0.0 2.3 %copy-start = (bf16[128,128]{1,0:T(8,128)(2,1)S(1)}, bf16[128,128]{1,0:T(8,128)(2,1)}, u32[]{:S(2)}) copy-start(bf16[128,128]{1,0:T(8,128)(2,1)} %param.13) | copy-start | bytes 98308
  0.0 1.1 %copy-start.1 = (bf16[16,32,128]{2,1,0:T(8,128)(2,1)S(1)}, bf16[16,32,128]{2,1,0:T(8,128)(2,1)}, u32[]{:S(2)}) copy-start(bf16[16,32,128]{2,1,0:T(8,128)(2,1)} %param.9) | copy-start | bytes 393220
  1.4 0.7 %copy-start.5 = (f32[128]{0:T(128)S(1)}, f32[128]{0:T(128)}, u32[]{:S(2)}) copy-start(f32[128]{0:T(128)} %param.10) | copy-start | bytes 1540
  2.3 0.8 %copy-start.2 = (bf16[128,128]{1,0:T(8,128)(2,1)S(1)}, bf16[128,128]{1,0:T(8,128)(2,1)}, u32[]{:S(2)}) copy-start(bf16[128,128]{1,0:T(8,128)(2,1)} %param.11) | copy-start | bytes 98308
  4.8 6.5 %copy-start.7 = (bf16[128,128]{1,0:T(8,128)(2,1)S(1)}, bf16[128,128]{1,0:T(8,128)(2,1)}, u32[]{:S(2)}) copy-start(bf16[128,128]{1,0:T(8,128)(2,1)} %param.14) | copy-start | bytes 98308
  4.8 13.2 %all-to-all-start.1 = ((bf16[4,2,8192]{2,1,0:T(2,128)(2,1)}), bf16[4,2,8192]{2,1,0:T(2,128)(2,1)S(1)}, u32[]{:S(2)}, u32[]{:S(2)}) async-start(bf16[4,2,8192]{2,1,0:T(2,128)(2,1)} %reshape.43), calls=%async_computation.1 | async-start | bytes 262144 | tf_op jit(solution)/shard_map/all_to_all | solution.py:62
  11.3 0.8 %copy-start.3 = (bf16[128,128]{1,0:T(8,128)(2,1)S(1)}, bf16[128,128]{1,0:T(8,128)(2,1)}, u32[]{:S(2)}) copy-start(bf16[128,128]{1,0:T(8,128)(2,1)} %param.12) | copy-start | bytes 98308
  18.0 9.2 %all-to-all-start = ((bf16[4,2,8192]{2,1,0:T(2,128)(2,1)}), bf16[4,2,8192]{2,1,0:T(2,128)(2,1)S(1)}, u32[]{:S(2)}, u32[]{:S(2)}) async-start(bf16[4,2,8192]{2,1,0:T(2,128)(2,1)} %reshape.41), calls=%async_computation | async-start | bytes 262144 | tf_op jit(solution)/shard_map/all_to_all | solution.py:63
  31.1 3.5 %copy-start.8 = (bf16[128,128]{1,0:T(8,128)(2,1)S(1)}, bf16[128,128]{1,0:T(8,128)(2,1)}, u32[]{:S(2)}) copy-start(bf16[128,128]{1,0:T(8,128)(2,1)} %param.17) | copy-start | bytes 98308
  31.1 10.1 %all-to-all-start.2 = ((bf16[4,2,8192]{2,1,0:T(2,128)(2,1)}), bf16[4,2,8192]{2,1,0:T(2,128)(2,1)S(1)}, u32[]{:S(2)}, u32[]{:S(2)}) async-start(bf16[4,2,8192]{2,1,0:T(2,128)(2,1)} %reshape.45), calls=%async_computation.2 | async-start | bytes 262144 | tf_op jit(solution)/shard_map/all_to_all | solution.py:71
  43.1 0.7 %copy-start.6 = (f32[128]{0:T(128)S(1)}, f32[128]{0:T(128)}, u32[]{:S(2)}) copy-start(f32[128]{0:T(128)} %param.15) | copy-start | bytes 1540
  43.8 0.8 %copy-start.4 = (bf16[128,128]{1,0:T(8,128)(2,1)S(1)}, bf16[128,128]{1,0:T(8,128)(2,1)}, u32[]{:S(2)}) copy-start(bf16[128,128]{1,0:T(8,128)(2,1)} %param.16) | copy-start | bytes 98308
where the time goes:
time: 46.2 us; the launch traced here: 45.4 us
  starting transfers between devices  13.3 us (29%)
  waiting for transfers between devices  12.7 us (27%)
  local copies, waits for them, and re-layouts  12.3 us (27%)
  other arithmetic  2.41 us (5%)
  matrix products  2.19 us (5%)
  blocking collectives  2.19 us (5%)
    unnamed x24, local copies, waits for them, and re-layouts  6.73 us
    all_to_all x1, starting transfers between devices, body(): lax.all_to_all(left, 'north', split_axis=2, concat_axis=0, tiled=True)  6.51 us
    all_to_all x1, waiting for transfers between devices, body(): lax.all_to_all(strip, 'north', split_axis=0, concat_axis=2, tiled=True)  6.41 us
    all_to_all x1, waiting for transfers between devices, body(): lax.all_to_all(left, 'north', split_axis=2, concat_axis=0, tiled=True)  4.13 us
    all_to_all x1, starting transfers between devices, body(): lax.all_to_all(strip, 'north', split_axis=0, concat_axis=2, tiled=True)  3.46 us
    all_to_all x1, starting transfers between devices, body(): lax.all_to_all(right, 'north', split_axis=2, concat_axis=0, tiled=True)  3.33 us
    all_gather x1, blocking collectives, over_all(): everything = lax.all_gather(piece, axis, axis=dim, tiled=True)  2.19 us
    all_to_all x1, waiting for transfers between devices, body(): lax.all_to_all(right, 'north', split_axis=2, concat_axis=0, tiled=True)  2.17 us
  transfers between devices with their start and end apart: 3, of which 3 were waited for; matrix products, arithmetic and copies ran while one was open for 8% of the time, Pallas kernels for 0%

commit v1 on v0

--- a/solution.py
+++ b/solution.py
@@ -1,6 +1,10 @@
+import functools
+
 import jax
 import jax.numpy as jnp
 from jax import lax
+from jax.experimental import pallas as pl
+from jax.experimental.pallas import tpu as pltpu
 from jax.sharding import PartitionSpec as P
 
 
@@ -72,6 +76,292 @@
     return finish_pair(mixed, ready, mid_gain, out_weight, out_gate)
 
 
+F32 = jnp.float32
+BF16 = jnp.bfloat16
+MESH = pl.DeviceIdType.MESH
+CHUNKS = 2
+GROUP = 8
+
+
+def logistic(values):
+    return 0.5 * jnp.tanh(0.5 * values) + 0.5
+
+
+def product(a, b):
+    return jnp.dot(a, b, preferred_element_type=F32)
+
+
+def fused_kernel(
+    north,
+    east,
+    pair_ref,
+    in_gain_ref,
+    left_weight_ref,
+    right_weight_ref,
+    left_gate_ref,
+    right_gate_ref,
+    mid_gain_ref,
+    out_weight_ref,
+    out_gate_ref,
+    out_ref,
+    left_own,
+    left_lines,
+    right_lines,
+    left_wide,
+    right_wide,
+    total,
+    gate_ref,
+    up_send,
+    down_send,
+    right_recv,
+    left_send,
+    left_recv,
+    pass_send,
+):
+    lines, cols, channels = pair_ref.shape
+    mix = left_weight_ref.shape[1]
+    blocks = cols // lines
+    n = lax.axis_index("north")
+    e = lax.axis_index("east")
+    partner = 1 - e
+    owner = n // blocks == e
+    half = lines // CHUNKS
+
+    barrier = pltpu.get_barrier_semaphore()
+    for flat in range(1, north * east):
+        other_n = lax.rem(n + flat // east, north)
+        other_e = lax.rem(e + flat % east, east)
+        pl.semaphore_signal(
+            barrier, inc=1, device_id={"north": other_n, "east": other_e}, device_id_type=MESH
+        )
+
+    rows = pair_ref[...].reshape(lines * cols, channels).astype(F32)
+    ready = scale_channels(rows, in_gain_ref[...]).astype(BF16)
+    right = product(ready, right_weight_ref[...]) * logistic(product(ready, right_gate_ref[...]))
+    right_lines[n] = right.astype(BF16).reshape(lines, cols, mix)
+    left = product(ready, left_weight_ref[...]) * logistic(product(ready, left_gate_ref[...]))
+    left = left.astype(BF16).reshape(lines, blocks, lines, mix)
+    for h in range(blocks):
+        left_own[h] = left[:, h]
+
+    pl.semaphore_wait(barrier, north * east - 1)
+
+    def line_copy(source, chunk, sends, target):
+        ref = right_lines.at[source, pl.ds(chunk * half, half)]
+        return pltpu.make_async_remote_copy(
+            src_ref=ref,
+            dst_ref=ref,
+            send_sem=sends.at[source, chunk],
+            recv_sem=right_recv.at[source, chunk],
+            device_id={"north": target},
+            device_id_type=MESH,
+        )
+
+    def up_copy(source, chunk):
+        return line_copy(source, chunk, up_send, jnp.minimum(n + 1, north - 1))
+
+    def down_copy(source, chunk):
+        return line_copy(source, chunk, down_send, jnp.maximum(n - 1, 0))
+
+    def left_copy(h):
+        return pltpu.make_async_remote_copy(
+            src_ref=left_own.at[h],
+            dst_ref=left_lines.at[n],
+            send_sem=left_send.at[h],
+            recv_sem=left_recv.at[n],
+            device_id={"north": e * blocks + h},
+            device_id_type=MESH,
+        )
+
+    def own_pass(h):
+        return pltpu.make_async_remote_copy(
+            src_ref=left_own.at[h],
+            dst_ref=left_lines.at[n],
+            send_sem=pass_send.at[n],
+            recv_sem=left_recv.at[n],
+            device_id={"east": partner},
+            device_id_type=MESH,
+        )
+
+    def pass_copy(source):
+        return pltpu.make_async_remote_copy(
+            src_ref=left_lines.at[source],
+            dst_ref=left_lines.at[source],
+            send_sem=pass_send.at[source],
+            recv_sem=left_recv.at[source],
+            device_id={"east": partner},
+            device_id_type=MESH,
+        )
+
+    for chunk in range(CHUNKS):
+        @pl.when(n < north - 1)
+        def _():
+            up_copy(n, chunk).start()
+
+        @pl.when(n > 0)
+        def _():
+            down_copy(n, chunk).start()
+
+    for h in range(blocks):
+        @pl.when(e * blocks + h == n)
+        def _():
+            own_pass(h).start()
+            left_lines[n] = left_own[h]
+
+        @pl.when(e * blocks + h != n)
+        def _():
+            left_copy(h).start()
+
+    gate_ref[...] = logistic(product(ready, out_gate_ref[...]))
+    total[...] = jnp.zeros_like(total)
+
+    def contract(source):
+        left_wide[...] = left_lines[source].astype(F32)
+        right_wide[...] = right_lines[source].astype(F32)
+
+        def group(g, carry):
+            base = pl.multiple_of(g * GROUP, GROUP)
+            sums = [total[base + i] for i in range(GROUP)]
+            for k in range(lines):
+                r = right_wide[k]
+                for i in range(GROUP):
+                    row = left_wide[k, pl.ds(base + i, 1), :]
+                    sums[i] = sums[i] + jnp.broadcast_to(row, r.shape) * r
+            for i in range(GROUP):
+                total[base + i] = sums[i]
+            return carry
+
+        lax.fori_loop(0, lines // GROUP, group, 0)
+
+    @pl.when(jnp.logical_not(owner))
+    def _():
+        pass_copy(n).wait_recv()
+
+    contract(n)
+
+    for step in range(1, north):
+        below, above = n - step, n + step
+        for chunk in range(CHUNKS):
+            @pl.when(below >= 0)
+            def _():
+                up_copy(below, chunk).wait_recv()
+
+                @pl.when(n < north - 1)
+                def _():
+                    up_copy(below, chunk).start()
+
+            @pl.when(above < north)
+            def _():
+                down_copy(above, chunk).wait_recv()
+
+                @pl.when(n > 0)
+                def _():
+                    down_copy(above, chunk).start()
+
+        for source in (below, above):
+            @pl.when(jnp.logical_and(source >= 0, source < north))
+            def _():
+                pass_copy(source).wait_recv()
+
+                @pl.when(owner)
+                def _():
+                    pass_copy(source).start()
+
+        for source in (below, above):
+            @pl.when(jnp.logical_and(source >= 0, source < north))
+            def _():
+                contract(source)
+
+    mixed = (total[...] * (lines * north) ** (-0.5)).astype(BF16).astype(F32)
+    mixed = mixed.reshape(lines * cols, mix)
+    scaled = scale_channels(mixed, mid_gain_ref[...]).astype(BF16)
+    out = product(scaled, out_weight_ref[...]) * gate_ref[...]
+    out_ref[...] = out.astype(BF16).reshape(lines, cols, channels)
+
+    for h in range(blocks):
+        @pl.when(e * blocks + h == n)
+        def _():
+            own_pass(h).wait_send()
+
+        @pl.when(e * blocks + h != n)
+        def _():
+            left_copy(h).wait_send()
+
+    for source in range(north):
+        @pl.when(jnp.logical_and(owner, source != n))
+        def _():
+            pass_copy(source).wait_send()
+
+        for chunk in range(CHUNKS):
+            @pl.when(jnp.logical_and(source <= n, n < north - 1))
+            def _():
+                up_copy(source, chunk).wait_send()
+
+            @pl.when(jnp.logical_and(source >= n, n > 0))
+            def _():
+                down_copy(source, chunk).wait_send()
+
+
+def fused_body(
+    pair_rows,
+    in_gain,
+    left_weight,
+    right_weight,
+    left_gate,
+    right_gate,
+    mid_gain,
+    out_weight,
+    out_gate,
+):
+    north, east = lax.axis_size("north"), lax.axis_size("east")
+    lines, cols, channels = pair_rows.shape
+    mix = left_weight.shape[1]
+    blocks = cols // lines
+    vmem = pl.BlockSpec(memory_space=pltpu.VMEM)
+    dma = pltpu.SemaphoreType.DMA
+    return pl.pallas_call(
+        functools.partial(fused_kernel, north, east),
+        out_shape=jax.ShapeDtypeStruct(pair_rows.shape, BF16),
+        in_specs=[vmem] * 9,
+        out_specs=vmem,
+        scratch_shapes=[
+            pltpu.VMEM((blocks, lines, lines, mix), BF16),
+            pltpu.VMEM((north, lines, lines, mix), BF16),
+            pltpu.VMEM((north, lines, cols, mix), BF16),
+            pltpu.VMEM((lines, lines, mix), F32),
+            pltpu.VMEM((lines, cols, mix), F32),
+            pltpu.VMEM((lines, cols, mix), F32),
+            pltpu.VMEM((lines * cols, channels), F32),
+            dma((north, CHUNKS)),
+            dma((north, CHUNKS)),
+            dma((north, CHUNKS)),
+            dma((blocks,)),
+            dma((north,)),
+            dma((north,)),
+        ],
+        compiler_params=pltpu.CompilerParams(collective_id=0, has_side_effects=True),
+    )(
+        pair_rows,
+        in_gain.reshape(1, -1),
+        left_weight,
+        right_weight,
+        left_gate,
+        right_gate,
+        mid_gain.reshape(1, -1),
+        out_weight,
+        out_gate,
+    )
+
+
+def choose_body(*args):
+    lines, cols, channels = args[0].shape
+    north, east = lax.axis_size("north"), lax.axis_size("east")
+    small = north * lines * (lines + cols) * args[2].shape[1] <= 2**21
+    if small and east == 2 and lines * north == cols * east and lines % 16 == 0:
+        return fused_body(*args)
+    return body(*args)
+
+
 def solution(mesh):
     placed = (
         P(("unit", "north"), "east", None),
@@ -85,7 +375,7 @@
         P("unit", None),
     )
     return jax.shard_map(
-        body,
+        choose_body,
         mesh=mesh,
         in_specs=placed,
         out_specs=P(("unit", "north"), "east", None),

time: 46.2 us -> 24.3 us (0.53)
  the two profiles are of different devices: /device:TPU:0 before, /device:TPU:1 now
where the time goes in v1:
time: 24.3 us; the launch traced here: 24.2 us
  Pallas kernels  22.6 us (93%)
  local copies, waits for them, and re-layouts  1.57 us (6%)
    pallas_call x1, Pallas kernels, fused_body(): pl.pallas_call(functools.partial(fused_kernel, north, east), out_shape=ja...  22.6 us
    unnamed x1, local copies, waits for them, and re-layouts  1.57 us

profile of v1, /device:TPU:1, one launch (start us, length us, event | category | flops | bytes accessed | tf_op | source)
XLA Modules:
  0.0 24.2 jit_solution(1018706730896660694)
XLA Ops:
  0.0 22.6 %shard_map.91 = bf16[16,32,128]{2,1,0:T(8,128)(2,1)} custom-call(bf16[16,32,128]{2,1,0:T(8,128)(2,1)} %pair_ref.1, f32[1,128]{1,0:T(1,128)} %bitcast.2, bf16[128,128]{1,0:T(8,128)(2,1)} %left_weight_ref.1, bf16[128,128]{1,0:T(8,128)(2,1)} %right_weight_ref.1, bf16[128,128]{1,0:T(8,128)(2,1)} %left_gate_ref.1, bf16[128,128]{1,0:T(8,128)(2,1)} %right_gate_ref.1, ...), custom_call_target="tpu_custom_call" | custom-call | tf_op jit(solution)/shard_map/pallas_call | solution.py:322
  22.6 1.6 %copy.11 = bf16[16,32,128]{2,1,0:T(8,128)(2,1)} copy(bf16[16,32,128]{2,1,0:T(8,128)(2,1)} %shard_map.91) | data formatting | bytes 262144
